TPU v7x, 32 devices: a whole 2x2x4 slice. The times are simulated.
32 devices in a mesh: segment: 4 (over x, core), dp: 8 (over z, y).
Axes of the slice: x: 2, y: 2, z: 4, core: 2. Of those that a mesh axis runs over, the one named last changes fastest.
Arguments:
- embeds: bfloat16 [2, 8, 128, 4096], P(None, 'dp'), may hold values from -6 to 6
- base_weight: bfloat16 [4, 4096, 4096], P('segment', 'dp'), may hold values from -0.09375 to 0.09375
- norm_gain: float32 [4, 4096], P('segment'), may hold values from 0.25 to 1.75
- skill_down: bfloat16 [4, 16, 8, 4096], P('segment'), may hold values from -0.09375 to 0.09375
- skill_up: bfloat16 [4, 16, 8, 4096], P('segment'), may hold values from -2 to 2
- task_ids: int32 [2, 8], replicated, may hold values from 0 to 1835
- allocation: int32 [1836, 16], replicated, may hold values 0 or 1
- target_lengths: int32 [2, 8], replicated, may hold values from 1 to 128
- cotangent: bfloat16 [2, 8, 128, 4096], P(None, 'dp'), may hold values from -6 to 6
Outputs:
- hidden: bfloat16 [4, 2, 8, 128, 4096], P('segment', None, 'dp')
- input_grads: bfloat16 [4, 2, 8, 128, 4096], P('segment', None, 'dp')
- grad_down: float32 [4, 16, 8, 4096], P('segment', None, None, 'dp')
- grad_up: float32 [4, 16, 8, 4096], P('segment', None, None, 'dp')
All inputs are finite; a program needn't handle non-finite values.
Results may differ from a plain program's by a relative error of at most 0.019.
Values may be sent and summed in bfloat16 or wider, within the bound.
No kernel may reach another device: no remote copies, remote signals or barrier semaphores. Data moves between devices by JAX's collectives and lax.ppermute only.
A program may use at most 192 MiB of HBM per device.

v0:
```python
import jax
import jax.numpy as jnp
from jax import lax
from jax.sharding import PartitionSpec as P

EPS = 1e-06


def shifted(block, axis, distance):
    devices = range(lax.axis_size(axis))
    route = [(i - distance, i) for i in devices if i - distance in devices]
    return lax.ppermute(block, axis, route)


def prepare(x, gain, down_t):
    xf = x.astype(jnp.float32)
    inv = lax.rsqrt(jnp.mean(xf * xf, axis=-1, keepdims=True) + EPS)
    normed = (xf * inv * gain).astype(jnp.bfloat16)
    low = jnp.dot(normed, down_t.T, preferred_element_type=jnp.float32).astype(jnp.bfloat16)
    return (normed, low, inv)


def forward_full(x, weight, gain, down_t, up_t):
    normed, low, inv = prepare(x, gain, down_t)
    total = x.astype(jnp.float32) + jnp.dot(normed, weight, preferred_element_type=jnp.float32)
    total = total + jnp.dot(low, up_t, preferred_element_type=jnp.float32)
    return (total.astype(jnp.bfloat16), normed, low, inv)


def backward_core(x, normed, low, inv, grad_out, weight, gain, down_t, up_t):
    g_low = jnp.dot(grad_out, up_t.T, preferred_element_type=jnp.float32).astype(jnp.bfloat16)
    dnorm = jnp.dot(grad_out, weight.T, preferred_element_type=jnp.float32)
    dnorm = dnorm + jnp.dot(g_low, down_t, preferred_element_type=jnp.float32)
    seq_down = jnp.dot(g_low.T, normed, preferred_element_type=jnp.float32)
    seq_up = jnp.dot(low.T, grad_out, preferred_element_type=jnp.float32)
    xf = x.astype(jnp.float32)
    scaled = gain * dnorm
    grad_in = (
        grad_out.astype(jnp.float32)
        + inv * scaled
        - xf * inv * inv * inv * jnp.mean(xf * scaled, axis=-1, keepdims=True)
    )
    return (grad_in.astype(jnp.bfloat16), seq_down, seq_up)


def pick(table, index):
    return lax.dynamic_index_in_dim(table, index, 0, keepdims=False)


def place(table, value, index, active):
    return jnp.where(active, lax.dynamic_update_index_in_dim(table, value, index, 0), table)


def shards(
    embeds,
    base_weight,
    norm_gain,
    skill_down,
    skill_up,
    task_ids,
    allocation,
    target_lengths,
    cotangent,
):
    segments = lax.axis_size("segment")
    segment = lax.axis_index("segment")
    member = lax.axis_index("dp")
    weight = lax.all_gather(base_weight[0], "dp", axis=0, tiled=True)
    gain = norm_gain[0]
    micro = embeds.shape[0]
    rows = embeds.shape[2]
    width = embeds.shape[3]
    splits = 1
    blocks = micro * splits
    block_rows = rows // splits
    tasks = lax.dynamic_index_in_dim(task_ids, member, 1, keepdims=False)
    lengths = lax.dynamic_index_in_dim(target_lengths, member, 1, keepdims=False)
    onehot = (tasks[:, None] == jnp.arange(allocation.shape[0], dtype=jnp.int32)[None, :]).astype(
        jnp.float32
    )
    alloc = allocation.astype(jnp.float32)
    counts = jnp.maximum(jnp.sum(alloc, axis=1, keepdims=True), 1.0)
    mix = jnp.einsum("mt,ts->ms", onehot, alloc / counts, precision=lax.Precision.HIGHEST)
    down_seq = jnp.einsum(
        "ms,srd->mrd", mix, skill_down[0].astype(jnp.float32), precision=lax.Precision.HIGHEST
    ).astype(jnp.bfloat16)
    up_seq = jnp.einsum(
        "ms,srd->mrd", mix, skill_up[0].astype(jnp.float32), precision=lax.Precision.HIGHEST
    ).astype(jnp.bfloat16)
    down_all = jnp.repeat(down_seq, splits, axis=0)
    up_all = jnp.repeat(up_seq, splits, axis=0)
    mix_all = jnp.repeat(mix, splits, axis=0)
    firsts = embeds[:, 0]
    live = jnp.arange(rows, dtype=jnp.int32)[None, :] < lengths[:, None]
    seeds = cotangent[:, 0] * live[..., None].astype(jnp.bfloat16)
    ticks = segments + blocks - 1
    rank = down_all.shape[1]
    blank = jnp.zeros((block_rows, width), jnp.bfloat16)
    stack_blank = jnp.zeros((blocks, block_rows, width), jnp.bfloat16)
    low_blank = jnp.zeros((blocks, block_rows, rank), jnp.bfloat16)
    inv_blank = jnp.zeros((blocks, block_rows, 1), jnp.float32)

    def forward_tick(tick, carry):
        incoming, saved, outs, kept_norm, kept_low, kept_inv = carry
        slot = tick - segment
        active = (slot >= 0) & (slot < blocks)
        index = jnp.clip(slot, 0, blocks - 1)
        x = jnp.where(segment == 0, pick(firsts, index), incoming)
        result, normed, low, inv = lax.cond(
            active,
            lambda: forward_full(x, weight, gain, pick(down_all, index), pick(up_all, index)),
            lambda: (
                blank,
                blank,
                jnp.zeros((block_rows, rank), jnp.bfloat16),
                jnp.zeros((block_rows, 1), jnp.float32),
            ),
        )
        saved = place(saved, x, index, active)
        outs = place(outs, result, index, active)
        return (result, (saved, outs, kept_norm, kept_low, kept_inv))

    def forward_step(tick, carry):
        result, rest = forward_tick(tick, carry)
        moved = shifted(result, "segment", 1)
        return (moved,) + rest

    carry = (blank, stack_blank, stack_blank, stack_blank, low_blank, inv_blank)
    carry = lax.fori_loop(0, ticks - 1, forward_step, carry)
    _, (saved, outs, kept_norm, kept_low, kept_inv) = forward_tick(ticks - 1, carry)
    skills = skill_down.shape[1]
    acc_blank = jnp.zeros((skills, rank, width), jnp.float32)

    def backward_tick(tick, carry):
        incoming, grads_in, acc_down, acc_up = carry
        slot = tick - (segments - 1 - segment)
        active = (slot >= 0) & (slot < blocks)
        index = jnp.clip(slot, 0, blocks - 1)
        grad_out = jnp.where(segment == segments - 1, pick(seeds, index), incoming)
        x = pick(saved, index)
        down_t = pick(down_all, index)
        up_t = pick(up_all, index)

        def run():
            normed, low, inv = prepare(x, gain, down_t)
            return backward_core(x, normed, low, inv, grad_out, weight, gain, down_t, up_t)

        grad_in, seq_down, seq_up = lax.cond(
            active,
            run,
            lambda: (
                blank,
                jnp.zeros((rank, width), jnp.float32),
                jnp.zeros((rank, width), jnp.float32),
            ),
        )
        weights = pick(mix_all, index)[:, None, None]
        acc_down = acc_down + weights * seq_down[None]
        acc_up = acc_up + weights * seq_up[None]
        grads_in = place(grads_in, grad_in, index, active)
        return (grad_in, (grads_in, acc_down, acc_up))

    def backward_step(tick, carry):
        grad_in, rest = backward_tick(tick, carry)
        moved = shifted(grad_in, "segment", -1)
        return (moved,) + rest

    carry = (blank, stack_blank, acc_blank, acc_blank)
    carry = lax.fori_loop(0, ticks - 1, backward_step, carry)
    _, (grads_in, acc_down, acc_up) = backward_tick(ticks - 1, carry)
    grad_down, grad_up = (
        lax.psum_scatter(
            acc_down.astype(jnp.bfloat16), "dp", scatter_dimension=2, tiled=True
        ).astype(jnp.float32),
        lax.psum_scatter(acc_up.astype(jnp.bfloat16), "dp", scatter_dimension=2, tiled=True).astype(
            jnp.float32
        ),
    )
    return (outs[None, :, None], grads_in[None, :, None], grad_down[None], grad_up[None])


def solution(mesh):
    in_specs = (
        P(None, "dp", None, None),
        P("segment", "dp", None),
        P("segment", None),
        P("segment", None, None, None),
        P("segment", None, None, None),
        P(),
        P(),
        P(),
        P(None, "dp", None, None),
    )
    out_specs = (
        P("segment", None, "dp", None, None),
        P("segment", None, "dp", None, None),
        P("segment", None, None, "dp"),
        P("segment", None, None, "dp"),
    )
    return jax.shard_map(shards, mesh=mesh, in_specs=in_specs, out_specs=out_specs, check_vma=False)
```

profile of v0, /device:TPU:0, one launch (start us, length us, event | category | flops | bytes accessed | tf_op | source)
XLA Modules:
  0.0 1101.7 jit_solution(8175166725081357591)
XLA Ops:
  10.2 2.8 convolution_convert_fusion.4
  16.1 633.9 %all-gather.3.cloned.1.call-done = bf16[1,4096,4096]{2,1,0:T(8,128)(2,1)} async-done(((bf16[1,512,4096]{2,1,0:T(8,128)(2,1)}), bf16[1,4096,4096]{2,1,0:T(8,128)(2,1)}) %all-gather.3.cloned.1.call-update) | async-done | bytes 33554448 | tf_op jit(solution)/shard_map/all_gather | solution.py:68
  652.9 111.1 %while.40 = (s32[]{:T(128)}, bf16[128,4096]{1,0:T(8,128)(2,1)}, bf16[2,128,4096]{2,1,0:T(8,128)(2,1)S(1)}, bf16[2,128,4096]{2,1,0:T(8,128)(2,1)}, s32[]{:T(128)}...) while((s32[]{:T(128)}, bf16[128,4096]{1,0:T(8,128)(2,1)}, ...), condition=%wide.region_5.6_spmd, body=%wide.region_1.5_spmd.sunk | while | flops 4321182720 | bytes 77762976 | solution.py:129
  656.1 18.8 %conditional.9 = (bf16[128,4096]{1,0:T(8,128)(2,1)S(1)}, bf16[1,128,4096]{2,1,0:T(8,128)(2,1)}) conditional(s32[]{:T(128)} %convert_element_type.342, () %tuple.144, (bf16[128,4096]{1,0:T(8,128)(2,1)S(1)}, f32[1,4096]{1,0:T(1,128)S(1)}, bf16[4096,4096]{1,0:T(8,128)(2,1)}, s32[]{:T(128)}, bf16[2,8,4096]{2,1,0:T(8,128)(2,1)S(1)}, ...), branch_computations={%region_2.2_spmd, %region_3.4_spmd} | conditional | flops 4319609856 | bytes 48401996 | solution.py:109
  656.4 13.0 %convolution_add_fusion.1 = f32[128,4096]{1,0:T(8,128)S(1)} fusion(bf16[4096,4096]{1,0:T(8,128)(2,1)} %get-tuple-element.684, bf16[128,4096]{1,0:T(8,128)(2,1)S(1)} %get-tuple-element.682, f32[4096]{0:T(1024)S(1)} %bitcast.180, f32[128]{0:T(128)S(1)} %add_rsqrt_fusion), kind=kOutput, calls=%fused_computation.1 | convolution fusion | flops 4298113024 | bytes 36717056 | tf_op jit(solution)/shard_map/while/body/eval_jaxpr/cond/branch_1_fun/dot_general | solution.py:25
  669.3 3.2 fusion
  677.4 2.8 select_dynamic-update-slice_fusion.4
  683.3 18.8 %conditional.9 = (bf16[128,4096]{1,0:T(8,128)(2,1)S(1)}, bf16[1,128,4096]{2,1,0:T(8,128)(2,1)}) conditional(s32[]{:T(128)} %convert_element_type.342, () %tuple.144, (bf16[128,4096]{1,0:T(8,128)(2,1)S(1)}, f32[1,4096]{1,0:T(1,128)S(1)}, bf16[4096,4096]{1,0:T(8,128)(2,1)}, s32[]{:T(128)}, bf16[2,8,4096]{2,1,0:T(8,128)(2,1)S(1)}, ...), branch_computations={%region_2.2_spmd, %region_3.4_spmd} | conditional | flops 4319609856 | bytes 48401996 | solution.py:109
  683.6 13.0 %convolution_add_fusion.1 = f32[128,4096]{1,0:T(8,128)S(1)} fusion(bf16[4096,4096]{1,0:T(8,128)(2,1)} %get-tuple-element.684, bf16[128,4096]{1,0:T(8,128)(2,1)S(1)} %get-tuple-element.682, f32[4096]{0:T(1024)S(1)} %bitcast.180, f32[128]{0:T(128)S(1)} %add_rsqrt_fusion), kind=kOutput, calls=%fused_computation.1 | convolution fusion | flops 4298113024 | bytes 36717056 | tf_op jit(solution)/shard_map/while/body/eval_jaxpr/cond/branch_1_fun/dot_general | solution.py:25
  696.6 3.2 fusion
  704.6 2.7 select_dynamic-update-slice_fusion.4
  711.7 28.8 %collective-permute-start = (bf16[128,4096]{1,0:T(8,128)(2,1)S(1)}, bf16[128,4096]{1,0:T(8,128)(2,1)}, u32[]{:S(2)}, u32[]{:S(2)}) collective-permute-start(bf16[128,4096]{1,0:T(8,128)(2,1)S(1)} %get-tuple-element.1077), channel_id=1, source_target_pairs={{0,8},{8,16},{16,24},{1,9},{9,17},{17,25},{2,10},{10,18},{18,26},{... | collective-permute-start | bytes 3145736 | tf_op jit(solution)/shard_map/while/body/eval_jaxpr/ppermute | solution.py:12
  747.3 14.2 %collective-permute-start = (bf16[128,4096]{1,0:T(8,128)(2,1)S(1)}, bf16[128,4096]{1,0:T(8,128)(2,1)}, u32[]{:S(2)}, u32[]{:S(2)}) collective-permute-start(bf16[128,4096]{1,0:T(8,128)(2,1)S(1)} %get-tuple-element.1077), channel_id=1, source_target_pairs={{0,8},{8,16},{16,24},{1,9},{9,17},{17,25},{2,10},{10,18},{18,26},{... | collective-permute-start | bytes 3145736 | tf_op jit(solution)/shard_map/while/body/eval_jaxpr/ppermute | solution.py:12
  764.0 2.8 fusion.140
  769.5 166.3 %while.41 = (s32[]{:T(128)}, bf16[128,4096]{1,0:T(8,128)(2,1)}, bf16[2,128,4096]{2,1,0:T(8,128)(2,1)}, f32[16,8,4096]{2,1,0:T(8,128)}, f32[16,8,4096]{2,1,0:T(8,...) while((s32[]{:T(128)}, bf16[128,4096]{1,0:T(8,128)(2,1)}, ...), condition=%wide.region_14.15_spmd.clone, body=%wide.region_9.14_spmd.clone.sunk | while | flops 4354214400 | bytes 94118616 | solution.py:169
  776.3 2.8 select_add_fusion.3
  779.1 25.7 %collective-permute-done.1 = bf16[128,4096]{1,0:T(8,128)(2,1)S(1)} collective-permute-done((bf16[128,4096]{1,0:T(8,128)(2,1)}, bf16[128,4096]{1,0:T(8,128)(2,1)S(1)}, u32[]{:S(2)}, u32[]{:S(2)}) %collective-permute-start.1) | collective-permute-done | bytes 1048608 | tf_op jit(solution)/shard_map/while/body/eval_jaxpr/ppermute | solution.py:12
  812.7 4.4 select_add_fusion.3
  817.0 8.2 collective-permute-done.1
  833.1 4.4 select_add_fusion.3
  837.5 53.9 %collective-permute-done.1 = bf16[128,4096]{1,0:T(8,128)(2,1)S(1)} collective-permute-done((bf16[128,4096]{1,0:T(8,128)(2,1)}, bf16[128,4096]{1,0:T(8,128)(2,1)S(1)}, u32[]{:S(2)}, u32[]{:S(2)}) %collective-permute-start.1) | collective-permute-done | bytes 1048608 | tf_op jit(solution)/shard_map/while/body/eval_jaxpr/ppermute | solution.py:12
  892.5 25.9 %conditional.10 = (bf16[128,4096]{1,0:T(8,128)(2,1)}, f32[8,4096]{1,0:T(8,128)S(1)}, f32[8,4096]{1,0:T(8,128)S(1)}, bf16[1,128,4096]{2,1,0:T(8,128)(2,1)}) conditional(s32[]{:T(128)} %convert_element_type.343, () %tuple.148, (pred[]{:T(512)}, bf16[2,128,4096]{2,1,0:T(8,128)(2,1)}, s32[]{:T(128)}, bf16[128,4096]{1,0:T(8,128)(2,1)}, ...), branch_computations={%region_10.10_spmd, %region_11.13_spmd} | conditional | flops 4350544384 | bytes 57155172 | solution.py:148
  895.4 16.0 %fusion.153 = f32[128,4096]{1,0:T(8,128)S(1)} fusion(bf16[128,4096]{1,0:T(8,128)(2,1)S(1)} %bitcast_select_fusion.2, bf16[4096,4096]{1,0:T(8,128)(2,1)} %get-tuple-element.714), kind=kOutput, calls=%fused_computation.166 | convolution fusion | flops 4294967296 | bytes 36700160 | tf_op jit(solution)/shard_map/while/body/eval_jaxpr/cond/branch_1_fun/dot_general | solution.py:32
  920.5 2.8 select_dynamic-update-slice_fusion.5
  923.3 4.4 select_add_fusion.3
  927.7 7.0 collective-permute-done.1
  935.8 22.5 %conditional.5 = (f32[8,4096]{1,0:T(8,128)S(1)}, f32[8,4096]{1,0:T(8,128)S(1)}, bf16[1,128,4096]{2,1,0:T(8,128)(2,1)}) conditional(s32[]{:T(128)} %convert_element_type.170, () %tuple.98, (pred[]{:T(512)}, bf16[2,128,4096]{2,1,0:T(8,128)(2,1)}, s32[]{:T(128)}, bf16[128,4096]{1,0:T(8,128)(2,1)}, bf16[2,8,4096]{2,0,1:T(2,128)(2,1)}, ...), branch_computations={%region_15.16_spmd, %region_16.19_spmd} | conditional | flops 4350544384 | bytes 56620128 | solution.py:148
  937.9 16.0 %fusion.154 = f32[128,4096]{1,0:T(8,128)S(1)} fusion(bf16[128,4096]{1,0:T(8,128)(2,1)S(1)} %bitcast_select_fusion.3, bf16[4096,4096]{1,0:T(8,128)(2,1)} %get-tuple-element.744), kind=kOutput, calls=%fused_computation.167 | convolution fusion | flops 4294967296 | bytes 36700160 | tf_op jit(solution)/shard_map/cond/branch_1_fun/dot_general | solution.py:32
  958.3 4.2 add_convert_fusion
  969.1 3.7 bitcast_dynamic-update-slice_fusion
  972.9 53.5 %reduce-scatter.5.cloned.1.call-done = bf16[16,8,512]{2,1,0:T(8,128)(2,1)} async-done(((bf16[16,8,4096]{2,1,0:T(8,128)(2,1)}), bf16[16,8,512]{2,1,0:T(8,128)(2,1)}) %reduce-scatter.5.cloned.1.call-update) | async-done | bytes 131088 | tf_op jit(solution)/shard_map/reduce_scatter | solution.py:175
  1028.0 65.5 %reduce-scatter.3.cloned.1.call-done = bf16[16,8,512]{2,1,0:T(8,128)(2,1)} async-done(((bf16[16,8,4096]{2,1,0:T(8,128)(2,1)}), bf16[16,8,512]{2,1,0:T(8,128)(2,1)}) %reduce-scatter.3.cloned.1.call-update) | async-done | bytes 131088 | tf_op jit(solution)/shard_map/reduce_scatter | solution.py:172
  (179 shorter events, 104.5 us)
Async XLA Ops:
  7.2 642.8 %all-gather.3.cloned.1.call-start = ((), (), s32[]{:S(2)}) async-start(), calls=%async_computation.4 | async-start | bytes 37748736 | tf_op jit(solution)/shard_map/all_gather | solution.py:68
  7.9 5.8 copy-start.25
  7.9 6.6 copy-start.12
  8.0 1018.4 %reduce-scatter.5.cloned.1.call-start = ((), (), s32[]{:S(2)}) async-start(), calls=%async_computation.3 | async-start | bytes 1179648 | tf_op jit(solution)/shard_map/reduce_scatter | solution.py:175
  8.5 7.6 copy-start.23
  10.1 6.0 copy-start.13
  13.0 3.1 copy-start.16
  674.9 5.3 copy-start.3
  674.9 5.3 collective-permute-start
  702.2 5.2 copy-start.3
  702.2 5.2 collective-permute-start
  711.7 31.3 %copy-start.3 = (bf16[2,128,4096]{2,1,0:T(8,128)(2,1)S(1)}, bf16[2,128,4096]{2,1,0:T(8,128)(2,1)}, u32[]{:S(2)}) copy-start(bf16[2,128,4096]{2,1,0:T(8,128)(2,1)} %copy-done.2) | copy-start | bytes 6291460 | tf_op jit(solution)/shard_map/while
  711.7 31.3 %collective-permute-start = (bf16[128,4096]{1,0:T(8,128)(2,1)S(1)}, bf16[128,4096]{1,0:T(8,128)(2,1)}, u32[]{:S(2)}, u32[]{:S(2)}) collective-permute-start(bf16[128,4096]{1,0:T(8,128)(2,1)S(1)} %get-tuple-element.1077), channel_id=1, source_target_pairs={{0,8},{8,16},{16,24},{1,9},{9,17},{17,25},{2,10},{10,18},{18,26},{... | collective-permute-start | bytes 3145736 | tf_op jit(solution)/shard_map/while/body/eval_jaxpr/ppermute | solution.py:12
  747.3 16.7 %copy-start.3 = (bf16[2,128,4096]{2,1,0:T(8,128)(2,1)S(1)}, bf16[2,128,4096]{2,1,0:T(8,128)(2,1)}, u32[]{:S(2)}) copy-start(bf16[2,128,4096]{2,1,0:T(8,128)(2,1)} %copy-done.2) | copy-start | bytes 6291460 | tf_op jit(solution)/shard_map/while
  747.3 16.7 %collective-permute-start = (bf16[128,4096]{1,0:T(8,128)(2,1)S(1)}, bf16[128,4096]{1,0:T(8,128)(2,1)}, u32[]{:S(2)}, u32[]{:S(2)}) collective-permute-start(bf16[128,4096]{1,0:T(8,128)(2,1)S(1)} %get-tuple-element.1077), channel_id=1, source_target_pairs={{0,8},{8,16},{16,24},{1,9},{9,17},{17,25},{2,10},{10,18},{18,26},{... | collective-permute-start | bytes 3145736 | tf_op jit(solution)/shard_map/while/body/eval_jaxpr/ppermute | solution.py:12
  771.7 33.0 %collective-permute-start.1 = (bf16[128,4096]{1,0:T(8,128)(2,1)}, bf16[128,4096]{1,0:T(8,128)(2,1)S(1)}, u32[]{:S(2)}, u32[]{:S(2)}) collective-permute-start(bf16[128,4096]{1,0:T(8,128)(2,1)} %get-tuple-element.1094), channel_id=1, source_target_pairs={{8,0},{16,8},{24,16},{9,1},{17,9},{25,17},{10,2},{18,10},{26,18},{... | collective-permute-start | bytes 3145736 | tf_op jit(solution)/shard_map/while/body/eval_jaxpr/ppermute | solution.py:12
  773.1 3.3 copy-start.5
  779.1 25.7 %copy-start.6 = (f32[16,8,4096]{2,1,0:T(8,128)}, f32[16,8,4096]{2,1,0:T(8,128)S(1)}, u32[]{:S(2)}) copy-start(f32[16,8,4096]{2,1,0:T(8,128)S(1)} %get-tuple-element.1191) | copy-start | bytes 6291460 | tf_op jit(solution)/shard_map/while
  808.1 17.2 %collective-permute-start.1 = (bf16[128,4096]{1,0:T(8,128)(2,1)}, bf16[128,4096]{1,0:T(8,128)(2,1)S(1)}, u32[]{:S(2)}, u32[]{:S(2)}) collective-permute-start(bf16[128,4096]{1,0:T(8,128)(2,1)} %get-tuple-element.1094), channel_id=1, source_target_pairs={{8,0},{16,8},{24,16},{9,1},{17,9},{25,17},{10,2},{18,10},{26,18},{... | collective-permute-start | bytes 3145736 | tf_op jit(solution)/shard_map/while/body/eval_jaxpr/ppermute | solution.py:12
  809.4 3.3 copy-start.5
  817.0 8.2 copy-start.6
  828.5 62.9 %collective-permute-start.1 = (bf16[128,4096]{1,0:T(8,128)(2,1)}, bf16[128,4096]{1,0:T(8,128)(2,1)S(1)}, u32[]{:S(2)}, u32[]{:S(2)}) collective-permute-start(bf16[128,4096]{1,0:T(8,128)(2,1)} %get-tuple-element.1094), channel_id=1, source_target_pairs={{8,0},{16,8},{24,16},{9,1},{17,9},{25,17},{10,2},{18,10},{26,18},{... | collective-permute-start | bytes 3145736 | tf_op jit(solution)/shard_map/while/body/eval_jaxpr/ppermute | solution.py:12
  829.8 3.3 copy-start.5
  837.5 53.9 %copy-start.6 = (f32[16,8,4096]{2,1,0:T(8,128)}, f32[16,8,4096]{2,1,0:T(8,128)S(1)}, u32[]{:S(2)}) copy-start(f32[16,8,4096]{2,1,0:T(8,128)S(1)} %get-tuple-element.1191) | copy-start | bytes 6291460 | tf_op jit(solution)/shard_map/while
  895.3 16.0 %copy-start.19 = (bf16[128,8]{0,1:T(8,128)(2,1)}, bf16[128,8]{0,1:T(8,128)(2,1)S(1)}, u32[]{:S(2)}) copy-start(bf16[128,8]{0,1:T(8,128)(2,1)S(1)} %convolution_convert_fusion.1) | copy-start | bytes 6148 | tf_op jit(solution)/shard_map/while/body/eval_jaxpr/cond
  912.2 4.1 copy-start.21
  918.4 16.3 %collective-permute-start.1 = (bf16[128,4096]{1,0:T(8,128)(2,1)}, bf16[128,4096]{1,0:T(8,128)(2,1)S(1)}, u32[]{:S(2)}, u32[]{:S(2)}) collective-permute-start(bf16[128,4096]{1,0:T(8,128)(2,1)} %get-tuple-element.1094), channel_id=1, source_target_pairs={{8,0},{16,8},{24,16},{9,1},{17,9},{25,17},{10,2},{18,10},{26,18},{... | collective-permute-start | bytes 3145736 | tf_op jit(solution)/shard_map/while/body/eval_jaxpr/ppermute | solution.py:12
  919.7 3.6 copy-start.5
  927.7 7.1 copy-start.6
  937.9 16.0 %copy-start.15 = (bf16[2,8,4096]{2,0,1:T(2,128)(2,1)S(1)}, bf16[2,8,4096]{2,0,1:T(2,128)(2,1)}, u32[]{:S(2)}) copy-start(bf16[2,8,4096]{2,0,1:T(2,128)(2,1)} %get-tuple-element.856) | copy-start | bytes 393220 | tf_op jit(solution)/shard_map/cond
  962.5 131.0 %reduce-scatter.3.cloned.1.call-start = ((), (), s32[]{:S(2)}) async-start(), calls=%async_computation.2 | async-start | bytes 1179648 | tf_op jit(solution)/shard_map/reduce_scatter | solution.py:172
  969.1 126.0 %copy-start.1 = (bf16[1,16,8,4096]{3,2,1,0:T(8,128)(2,1)S(1)}, bf16[1,16,8,4096]{3,2,1,0:T(8,128)(2,1)}, u32[]{:S(2)}) copy-start(bf16[1,16,8,4096]{3,2,1,0:T(8,128)(2,1)} %param.24) | copy-start | bytes 3145732
  (20 other events, 33.7 us)
Sparse Core Ops, SparseCore 0:
  9.5 640.3 all-gather.2
  962.6 63.6 reduce-scatter.4
  1029.8 63.6 reduce-scatter.2
where the time goes:
time: 1100 us
  waiting for transfers between devices  849 us (77%)
  matrix products  75.6 us (7%)
  other arithmetic  66.7 us (6%)
  starting transfers between devices  53.3 us (5%)
  local copies, waits for them, and re-layouts  42.4 us (4%)
  between operations  14 us (1%)
    all_gather x1, waiting for transfers between devices, shards(): weight = lax.all_gather(base_weight[0], 'dp', axis=0, tiled=True)  634 us
    ppermute x8, waiting for transfers between devices, shifted(): return lax.ppermute(block, axis, route)  94.9 us
    reduce_scatter x1, waiting for transfers between devices, shards(): lax.psum_scatter(acc_down.astype(jnp.bfloat16), 'dp', scatter_dimension=2...  65.5 us
    reduce_scatter x1, waiting for transfers between devices, shards(): lax.psum_scatter(acc_up.astype(jnp.bfloat16), 'dp', scatter_dimension=2,...  53.5 us
    ppermute x8, starting transfers between devices, shifted(): return lax.ppermute(block, axis, route)  53.2 us
    select_n x14, other arithmetic, place(): jnp.where(active, lax.dynamic_update_index_in_dim(table, value, index, 0)...  34.3 us
    dot_general x2, matrix products, backward_core(): dnorm = jnp.dot(grad_out, weight.T, preferred_element_type=jnp.float32)  32 us
    dot_general x2, matrix products, forward_full(): jnp.dot(normed, weight, preferred_element_type=jnp.float32)  25.9 us
  transfers between devices with their start and end apart: 11, of which 7 were waited for; matrix products, arithmetic and copies ran while one was open for 5% of the time, Pallas kernels for 0%

commit v1 on v0

--- a/solution.py
+++ b/solution.py
@@ -1,9 +1,28 @@
+import functools
 import jax
 import jax.numpy as jnp
 from jax import lax
 from jax.sharding import PartitionSpec as P
+from jax.lax import axis_index, axis_size, ppermute
 
 EPS = 1e-06
+
+
+def derive_targets(array_here, group_axis, k_dim):
+    history = []
+    nd = axis_size(group_axis)
+    for c in [*range(nd)]:
+        history.append((c, (c + 1) % nd))
+    x_now = [None] * nd
+    x_now[nd - 1] = array_here
+    for dev_i in range(nd - 2, -1, -1):
+        x_now[dev_i] = ppermute(x_now[dev_i + 1], group_axis, history)
+    e_now = jnp.concatenate(x_now, axis=k_dim)
+    r2 = axis_index(group_axis)
+    return jnp.roll(e_now, shift=(r2 + 1) * array_here.shape[k_dim], axis=k_dim)
+
+
+rails_try_all = functools.partial(derive_targets, group_axis="dp", k_dim=0)
 
 
 def shifted(block, axis, distance):
@@ -65,7 +84,7 @@
     segments = lax.axis_size("segment")
     segment = lax.axis_index("segment")
     member = lax.axis_index("dp")
-    weight = lax.all_gather(base_weight[0], "dp", axis=0, tiled=True)
+    weight = rails_try_all(base_weight[0])
     gain = norm_gain[0]
     micro = embeds.shape[0]
     rows = embeds.shape[2]

time: 1100 us -> 1200 us (1.091)
  local copies, waits for them, and re-layouts: 42.4 us -> 135 us
    ppermute x0 -> x7, waiting for transfers between devices: none -> 637 us  [derive_targets(): x_now[dev_i] = ppermute(x_now[dev_i + 1], group_axis, history)]
    all_gather x1 -> x0, waiting for transfers between devices: 634 us -> none  [shards(): weight = lax.all_gather(base_weight[0], 'dp', axis=0, tiled=True)]
    unnamed x32 -> x65, local copies, waits for them, and re-layouts: 4.84 us -> 65.9 us
    dynamic_slice x0 -> x1, local copies, waits for them, and re-layouts: none -> 22.9 us  [derive_targets(): return jnp.roll(e_now, shift=(r2 + 1) * array_here.shape[k_dim], axis=k_dim)]
  transfers between devices with their start and end apart: 11 -> 17, of which waited for: 7 -> 13; matrix products, arithmetic and copies ran while one was open for 5% -> 5% of each run, Pallas kernels for 0% -> 0%
where the time goes in v1:
time: 1200 us
  waiting for transfers between devices  848 us (71%)
  local copies, waits for them, and re-layouts  135 us (11%)
  matrix products  75.4 us (6%)
  other arithmetic  69.4 us (6%)
  starting transfers between devices  54.7 us (5%)
  between operations  14.2 us (1%)
    ppermute x7, waiting for transfers between devices, derive_targets(): x_now[dev_i] = ppermute(x_now[dev_i + 1], group_axis, history)  637 us
    ppermute x8, waiting for transfers between devices, shifted(): return lax.ppermute(block, axis, route)  94.9 us
    unnamed x65, local copies, waits for them, and re-layouts  65.9 us
    reduce_scatter x1, waiting for transfers between devices, shards(): lax.psum_scatter(acc_down.astype(jnp.bfloat16), 'dp', scatter_dimension=2...  65.5 us
    ppermute x8, starting transfers between devices, shifted(): return lax.ppermute(block, axis, route)  51.5 us
    reduce_scatter x1, waiting for transfers between devices, shards(): lax.psum_scatter(acc_up.astype(jnp.bfloat16), 'dp', scatter_dimension=2,...  49.9 us
    select_n x14, other arithmetic, place(): jnp.where(active, lax.dynamic_update_index_in_dim(table, value, index, 0)...  34.8 us
    dot_general x2, matrix products, backward_core(): dnorm = jnp.dot(grad_out, weight.T, preferred_element_type=jnp.float32)  32 us
  transfers between devices with their start and end apart: 17, of which 13 were waited for; matrix products, arithmetic and copies ran while one was open for 5% of the time, Pallas kernels for 0%

profile of v1, /device:TPU:0, one launch (start us, length us, event | category | flops | bytes accessed | tf_op | source)
XLA Modules:
  0.0 1197.9 jit_solution(15139325679225208291)
XLA Ops:
  10.3 93.8 %collective-permute-done.2 = bf16[512,4096]{1,0:T(8,128)(2,1)S(1)} collective-permute-done((bf16[512,4096]{1,0:T(8,128)(2,1)}, bf16[512,4096]{1,0:T(8,128)(2,1)S(1)}, u32[]{:S(2)}, u32[]{:S(2)}) %collective-permute-start.2) | collective-permute-done | bytes 4194336 | tf_op jit(solution)/shard_map/ppermute | solution.py:19
  106.2 94.4 %collective-permute-done.3 = bf16[512,4096]{1,0:T(8,128)(2,1)S(1)} collective-permute-done((bf16[512,4096]{1,0:T(8,128)(2,1)S(1)}, bf16[512,4096]{1,0:T(8,128)(2,1)S(1)}, u32[]{:S(2)}, u32[]{:S(2)}) %collective-permute-start.3) | collective-permute-done | bytes 4194336 | tf_op jit(solution)/shard_map/ppermute | solution.py:19
  202.6 93.6 %collective-permute-done.4 = bf16[512,4096]{1,0:T(8,128)(2,1)S(1)} collective-permute-done((bf16[512,4096]{1,0:T(8,128)(2,1)S(1)}, bf16[512,4096]{1,0:T(8,128)(2,1)S(1)}, u32[]{:S(2)}, u32[]{:S(2)}) %collective-permute-start.4) | collective-permute-done | bytes 4194336 | tf_op jit(solution)/shard_map/ppermute | solution.py:19
  298.1 92.7 %collective-permute-done.5 = bf16[512,4096]{1,0:T(8,128)(2,1)S(1)} collective-permute-done((bf16[512,4096]{1,0:T(8,128)(2,1)S(1)}, bf16[512,4096]{1,0:T(8,128)(2,1)S(1)}, u32[]{:S(2)}, u32[]{:S(2)}) %collective-permute-start.5) | collective-permute-done | bytes 4194336 | tf_op jit(solution)/shard_map/ppermute | solution.py:19
  392.8 91.9 %collective-permute-done.6 = bf16[512,4096]{1,0:T(8,128)(2,1)S(1)} collective-permute-done((bf16[512,4096]{1,0:T(8,128)(2,1)S(1)}, bf16[512,4096]{1,0:T(8,128)(2,1)S(1)}, u32[]{:S(2)}, u32[]{:S(2)}) %collective-permute-start.6) | collective-permute-done | bytes 4194336 | tf_op jit(solution)/shard_map/ppermute | solution.py:19
  486.7 91.1 %collective-permute-done.7 = bf16[512,4096]{1,0:T(8,128)(2,1)} collective-permute-done((bf16[512,4096]{1,0:T(8,128)(2,1)S(1)}, bf16[512,4096]{1,0:T(8,128)(2,1)}, u32[]{:S(2)}, u32[]{:S(2)}) %collective-permute-start.7) | collective-permute-done | bytes 4194336 | tf_op jit(solution)/shard_map/ppermute | solution.py:19
  588.7 79.6 %collective-permute-done.8 = bf16[512,4096]{1,0:T(8,128)(2,1)} collective-permute-done((bf16[512,4096]{1,0:T(8,128)(2,1)}, bf16[512,4096]{1,0:T(8,128)(2,1)}, u32[]{:S(2)}, u32[]{:S(2)}) %collective-permute-start.8) | collective-permute-done | bytes 4194336 | tf_op jit(solution)/shard_map/ppermute | solution.py:19
  668.3 4.6 constant_dynamic-update-slice_fusion.15
  672.9 4.9 constant_dynamic-update-slice_fusion.14
  698.6 4.7 constant_dynamic-update-slice_fusion.7
  703.3 4.7 constant_dynamic-update-slice_fusion.6
  721.6 22.9 %constant_dynamic-slice_fusion.4 = bf16[4096,4096]{1,0:T(8,128)(2,1)} fusion(bf16[8192,4096]{1,0:T(8,128)(2,1)} %constant_dynamic-update-slice_fusion, s32[]{:T(128)S(6)} %select_n.179), kind=kLoop, calls=%fused_computation.176 | loop fusion | bytes 67108864 | tf_op jit(solution)/shard_map/jit(_roll_dynamic)/dynamic_slice | solution.py:22
  747.4 115.8 %while.40 = (s32[]{:T(128)}, bf16[128,4096]{1,0:T(8,128)(2,1)}, bf16[2,128,4096]{2,1,0:T(8,128)(2,1)S(1)}, bf16[2,128,4096]{2,1,0:T(8,128)(2,1)}, s32[]{:T(128)}...) while((s32[]{:T(128)}, bf16[128,4096]{1,0:T(8,128)(2,1)}, ...), condition=%wide.region_5.6_spmd, body=%wide.region_1.5_spmd.sunk | while | flops 4321182720 | bytes 77762976 | solution.py:148
  750.6 18.8 %conditional.9 = (bf16[128,4096]{1,0:T(8,128)(2,1)}, bf16[1,128,4096]{2,1,0:T(8,128)(2,1)}) conditional(s32[]{:T(128)} %convert_element_type.342, () %tuple.144, (bf16[128,4096]{1,0:T(8,128)(2,1)S(1)}, f32[1,4096]{1,0:T(1,128)S(1)}, bf16[4096,4096]{1,0:T(8,128)(2,1)}, s32[]{:T(128)}, bf16[2,8,4096]{2,1,0:T(8,128)(2,1)S(1)}, ...), branch_computations={%region_2.2_spmd, %region_3.4_spmd} | conditional | flops 4319609856 | bytes 44207664 | solution.py:128
  750.9 13.0 %convolution_add_fusion.1 = f32[128,4096]{1,0:T(8,128)S(1)} fusion(bf16[4096,4096]{1,0:T(8,128)(2,1)} %get-tuple-element.684, bf16[128,4096]{1,0:T(8,128)(2,1)S(1)} %get-tuple-element.682, f32[4096]{0:T(1024)S(1)} %bitcast.181, f32[128]{0:T(128)S(1)} %add_rsqrt_fusion), kind=kOutput, calls=%fused_computation.1 | convolution fusion | flops 4298113024 | bytes 36717056 | tf_op jit(solution)/shard_map/while/body/eval_jaxpr/cond/branch_1_fun/dot_general | solution.py:44
  777.8 18.8 %conditional.9 = (bf16[128,4096]{1,0:T(8,128)(2,1)}, bf16[1,128,4096]{2,1,0:T(8,128)(2,1)}) conditional(s32[]{:T(128)} %convert_element_type.342, () %tuple.144, (bf16[128,4096]{1,0:T(8,128)(2,1)S(1)}, f32[1,4096]{1,0:T(1,128)S(1)}, bf16[4096,4096]{1,0:T(8,128)(2,1)}, s32[]{:T(128)}, bf16[2,8,4096]{2,1,0:T(8,128)(2,1)S(1)}, ...), branch_computations={%region_2.2_spmd, %region_3.4_spmd} | conditional | flops 4319609856 | bytes 44207664 | solution.py:128
  778.1 13.0 %convolution_add_fusion.1 = f32[128,4096]{1,0:T(8,128)S(1)} fusion(bf16[4096,4096]{1,0:T(8,128)(2,1)} %get-tuple-element.684, bf16[128,4096]{1,0:T(8,128)(2,1)S(1)} %get-tuple-element.682, f32[4096]{0:T(1024)S(1)} %bitcast.181, f32[128]{0:T(128)S(1)} %add_rsqrt_fusion), kind=kOutput, calls=%fused_computation.1 | convolution fusion | flops 4298113024 | bytes 36717056 | tf_op jit(solution)/shard_map/while/body/eval_jaxpr/cond/branch_1_fun/dot_general | solution.py:44
  808.3 28.2 %collective-permute-start = (bf16[128,4096]{1,0:T(8,128)(2,1)}, bf16[128,4096]{1,0:T(8,128)(2,1)S(1)}, u32[]{:S(2)}, u32[]{:S(2)}) collective-permute-start(bf16[128,4096]{1,0:T(8,128)(2,1)} %get-tuple-element.1077), channel_id=1, source_target_pairs={{0,8},{8,16},{16,24},{1,9},{9,17},{17,25},{2,10},{10,18},{18,26},{... | collective-permute-start | bytes 3145736 | tf_op jit(solution)/shard_map/while/body/eval_jaxpr/ppermute | solution.py:31
  845.4 14.3 %collective-permute-start = (bf16[128,4096]{1,0:T(8,128)(2,1)}, bf16[128,4096]{1,0:T(8,128)(2,1)S(1)}, u32[]{:S(2)}, u32[]{:S(2)}) collective-permute-start(bf16[128,4096]{1,0:T(8,128)(2,1)} %get-tuple-element.1077), channel_id=1, source_target_pairs={{0,8},{8,16},{16,24},{1,9},{9,17},{17,25},{2,10},{10,18},{18,26},{... | collective-permute-start | bytes 3145736 | tf_op jit(solution)/shard_map/while/body/eval_jaxpr/ppermute | solution.py:31
  868.7 166.1 %while.41 = (s32[]{:T(128)}, bf16[128,4096]{1,0:T(8,128)(2,1)}, bf16[2,128,4096]{2,1,0:T(8,128)(2,1)}, f32[16,8,4096]{2,1,0:T(8,128)}, f32[16,8,4096]{2,1,0:T(8,...) while((s32[]{:T(128)}, bf16[128,4096]{1,0:T(8,128)(2,1)}, ...), condition=%wide.region_14.15_spmd.clone, body=%wide.region_9.14_spmd.clone.sunk | while | flops 4354214400 | bytes 94118616 | solution.py:188
  878.3 25.7 %collective-permute-done.1 = bf16[128,4096]{1,0:T(8,128)(2,1)S(1)} collective-permute-done((bf16[128,4096]{1,0:T(8,128)(2,1)}, bf16[128,4096]{1,0:T(8,128)(2,1)S(1)}, u32[]{:S(2)}, u32[]{:S(2)}) %collective-permute-start.1) | collective-permute-done | bytes 1048608 | tf_op jit(solution)/shard_map/while/body/eval_jaxpr/ppermute | solution.py:31
  911.9 4.3 select_add_fusion.3
  916.2 8.1 collective-permute-done.1
  932.2 4.3 select_add_fusion.3
  936.5 54.0 %collective-permute-done.1 = bf16[128,4096]{1,0:T(8,128)(2,1)S(1)} collective-permute-done((bf16[128,4096]{1,0:T(8,128)(2,1)}, bf16[128,4096]{1,0:T(8,128)(2,1)S(1)}, u32[]{:S(2)}, u32[]{:S(2)}) %collective-permute-start.1) | collective-permute-done | bytes 1048608 | tf_op jit(solution)/shard_map/while/body/eval_jaxpr/ppermute | solution.py:31
  991.5 26.0 %conditional.10 = (bf16[128,4096]{1,0:T(8,128)(2,1)}, f32[8,4096]{1,0:T(8,128)S(1)}, f32[8,4096]{1,0:T(8,128)S(1)}, bf16[1,128,4096]{2,1,0:T(8,128)(2,1)}) conditional(s32[]{:T(128)} %convert_element_type.343, () %tuple.148, (pred[]{:T(512)}, bf16[2,128,4096]{2,1,0:T(8,128)(2,1)}, s32[]{:T(128)}, bf16[128,4096]{1,0:T(8,128)(2,1)}, ...), branch_computations={%region_10.10_spmd, %region_11.13_spmd} | conditional | flops 4350544384 | bytes 57155172 | solution.py:167
  994.4 16.0 %fusion.153 = f32[128,4096]{1,0:T(8,128)S(1)} fusion(bf16[128,4096]{1,0:T(8,128)(2,1)S(1)} %bitcast_select_fusion.2, bf16[4096,4096]{1,0:T(8,128)(2,1)} %get-tuple-element.714), kind=kOutput, calls=%fused_computation.183 | convolution fusion | flops 4294967296 | bytes 36700160 | tf_op jit(solution)/shard_map/while/body/eval_jaxpr/cond/branch_1_fun/dot_general | solution.py:51
  1026.7 7.1 collective-permute-done.1
  1034.8 22.6 %conditional.5 = (f32[8,4096]{1,0:T(8,128)S(1)}, f32[8,4096]{1,0:T(8,128)S(1)}, bf16[1,128,4096]{2,1,0:T(8,128)(2,1)}) conditional(s32[]{:T(128)} %convert_element_type.170, () %tuple.98, (pred[]{:T(512)}, bf16[2,128,4096]{2,1,0:T(8,128)(2,1)}, s32[]{:T(128)}, bf16[128,4096]{1,0:T(8,128)(2,1)}, bf16[2,8,4096]{2,0,1:T(2,128)(2,1)}, ...), branch_computations={%region_15.16_spmd, %region_16.19_spmd} | conditional | flops 4350544384 | bytes 56620128 | solution.py:167
  1037.0 16.0 %fusion.154 = f32[128,4096]{1,0:T(8,128)S(1)} fusion(bf16[128,4096]{1,0:T(8,128)(2,1)S(1)} %bitcast_select_fusion.3, bf16[4096,4096]{1,0:T(8,128)(2,1)} %get-tuple-element.744), kind=kOutput, calls=%fused_computation.184 | convolution fusion | flops 4294967296 | bytes 36700160 | tf_op jit(solution)/shard_map/cond/branch_1_fun/dot_general | solution.py:51
  1072.4 49.9 %reduce-scatter.5.cloned.1.call-done = bf16[16,8,512]{2,1,0:T(8,128)(2,1)} async-done(((bf16[16,8,4096]{2,1,0:T(8,128)(2,1)}), bf16[16,8,512]{2,1,0:T(8,128)(2,1)}) %reduce-scatter.5.cloned.1.call-update) | async-done | bytes 131088 | tf_op jit(solution)/shard_map/reduce_scatter | solution.py:194
  1123.9 65.5 %reduce-scatter.3.cloned.1.call-done = bf16[16,8,512]{2,1,0:T(8,128)(2,1)} async-done(((bf16[16,8,4096]{2,1,0:T(8,128)(2,1)}), bf16[16,8,512]{2,1,0:T(8,128)(2,1)}) %reduce-scatter.3.cloned.1.call-update) | async-done | bytes 131088 | tf_op jit(solution)/shard_map/reduce_scatter | solution.py:191
  (229 shorter events, 197.3 us)
Async XLA Ops:
  7.2 573.6 %copy-start = (bf16[1,16,8,4096]{3,2,1,0:T(8,128)(2,1)S(1)}, bf16[1,16,8,4096]{3,2,1,0:T(8,128)(2,1)}, u32[]{:S(2)}) copy-start(bf16[1,16,8,4096]{3,2,1,0:T(8,128)(2,1)} %param.24) | copy-start | bytes 3145732
  7.2 575.3 %copy-start.29 = (bf16[1,16,8,4096]{3,2,1,0:T(8,128)(2,1)S(1)}, bf16[1,16,8,4096]{3,2,1,0:T(8,128)(2,1)}, u32[]{:S(2)}) copy-start(bf16[1,16,8,4096]{3,2,1,0:T(8,128)(2,1)} %param.25) | copy-start | bytes 3145732
  7.2 577.6 %copy-start.34 = (s32[2,8]{1,0:T(2,128)S(1)}, s32[2,8]{1,0:T(2,128)}, u32[]{:S(2)}) copy-start(s32[2,8]{1,0:T(2,128)} %param.28) | copy-start | bytes 196
  7.2 1115.1 %reduce-scatter.5.cloned.1.call-start = ((), (), s32[]{:S(2)}) async-start(), calls=%async_computation.3 | async-start | bytes 1179648 | tf_op jit(solution)/shard_map/reduce_scatter | solution.py:194
  7.2 96.9 %collective-permute-start.2 = (bf16[512,4096]{1,0:T(8,128)(2,1)}, bf16[512,4096]{1,0:T(8,128)(2,1)S(1)}, u32[]{:S(2)}, u32[]{:S(2)}) collective-permute-start(bf16[512,4096]{1,0:T(8,128)(2,1)} %bitcast.180), channel_id=1, source_target_pairs={{0,1},{1,2},{2,3},{3,4},{4,5},{5,6},{6,7},{7,0},{8,9},{9,10},{10,1... | collective-permute-start | bytes 12582920 | tf_op jit(solution)/shard_map/ppermute | solution.py:19
  106.1 94.4 %collective-permute-start.3 = (bf16[512,4096]{1,0:T(8,128)(2,1)S(1)}, bf16[512,4096]{1,0:T(8,128)(2,1)S(1)}, u32[]{:S(2)}, u32[]{:S(2)}) collective-permute-start(bf16[512,4096]{1,0:T(8,128)(2,1)S(1)} %collective-permute-done.2), channel_id=1, source_target_pairs={{0,1},{1,2},{2,3},{3,4},{4,5},{5,6},{6,7},{7,0},{8,9},{9,10},{10,1... | collective-permute-start | bytes 12582920 | tf_op jit(solution)/shard_map/ppermute | solution.py:19
  202.6 93.6 %collective-permute-start.4 = (bf16[512,4096]{1,0:T(8,128)(2,1)S(1)}, bf16[512,4096]{1,0:T(8,128)(2,1)S(1)}, u32[]{:S(2)}, u32[]{:S(2)}) collective-permute-start(bf16[512,4096]{1,0:T(8,128)(2,1)S(1)} %collective-permute-done.3), channel_id=1, source_target_pairs={{0,1},{1,2},{2,3},{3,4},{4,5},{5,6},{6,7},{7,0},{8,9},{9,10},{10,1... | collective-permute-start | bytes 12582920 | tf_op jit(solution)/shard_map/ppermute | solution.py:19
  298.1 92.7 %collective-permute-start.5 = (bf16[512,4096]{1,0:T(8,128)(2,1)S(1)}, bf16[512,4096]{1,0:T(8,128)(2,1)S(1)}, u32[]{:S(2)}, u32[]{:S(2)}) collective-permute-start(bf16[512,4096]{1,0:T(8,128)(2,1)S(1)} %collective-permute-done.4), channel_id=1, source_target_pairs={{0,1},{1,2},{2,3},{3,4},{4,5},{5,6},{6,7},{7,0},{8,9},{9,10},{10,1... | collective-permute-start | bytes 12582920 | tf_op jit(solution)/shard_map/ppermute | solution.py:19
  392.8 91.9 %collective-permute-start.6 = (bf16[512,4096]{1,0:T(8,128)(2,1)S(1)}, bf16[512,4096]{1,0:T(8,128)(2,1)S(1)}, u32[]{:S(2)}, u32[]{:S(2)}) collective-permute-start(bf16[512,4096]{1,0:T(8,128)(2,1)S(1)} %collective-permute-done.5), channel_id=1, source_target_pairs={{0,1},{1,2},{2,3},{3,4},{4,5},{5,6},{6,7},{7,0},{8,9},{9,10},{10,1... | collective-permute-start | bytes 12582920 | tf_op jit(solution)/shard_map/ppermute | solution.py:19
  486.7 91.1 %collective-permute-start.7 = (bf16[512,4096]{1,0:T(8,128)(2,1)S(1)}, bf16[512,4096]{1,0:T(8,128)(2,1)}, u32[]{:S(2)}, u32[]{:S(2)}) collective-permute-start(bf16[512,4096]{1,0:T(8,128)(2,1)S(1)} %collective-permute-done.6), channel_id=1, source_target_pairs={{0,1},{1,2},{2,3},{3,4},{4,5},{5,6},{6,7},{7,0},{8,9},{9,10},{10,1... | collective-permute-start | bytes 12582920 | tf_op jit(solution)/shard_map/ppermute | solution.py:19
  577.8 90.5 %collective-permute-start.8 = (bf16[512,4096]{1,0:T(8,128)(2,1)}, bf16[512,4096]{1,0:T(8,128)(2,1)}, u32[]{:S(2)}, u32[]{:S(2)}) collective-permute-start(bf16[512,4096]{1,0:T(8,128)(2,1)} %collective-permute-done.7), channel_id=1, source_target_pairs={{0,1},{1,2},{2,3},{3,4},{4,5},{5,6},{6,7},{7,0},{8,9},{9,10},{10,1... | collective-permute-start | bytes 12582920 | tf_op jit(solution)/shard_map/ppermute | solution.py:19
  580.7 8.0 copy-start.33
  582.4 6.4 copy-start.23
  769.4 4.3 collective-permute-start
  796.7 6.2 copy-start.3
  796.7 5.2 collective-permute-start
  808.3 31.7 %copy-start.3 = (bf16[2,128,4096]{2,1,0:T(8,128)(2,1)S(1)}, bf16[2,128,4096]{2,1,0:T(8,128)(2,1)}, u32[]{:S(2)}) copy-start(bf16[2,128,4096]{2,1,0:T(8,128)(2,1)} %copy-done.2) | copy-start | bytes 6291460 | tf_op jit(solution)/shard_map/while
  808.3 30.7 %collective-permute-start = (bf16[128,4096]{1,0:T(8,128)(2,1)}, bf16[128,4096]{1,0:T(8,128)(2,1)S(1)}, u32[]{:S(2)}, u32[]{:S(2)}) collective-permute-start(bf16[128,4096]{1,0:T(8,128)(2,1)} %get-tuple-element.1077), channel_id=1, source_target_pairs={{0,8},{8,16},{16,24},{1,9},{9,17},{17,25},{2,10},{10,18},{18,26},{... | collective-permute-start | bytes 3145736 | tf_op jit(solution)/shard_map/while/body/eval_jaxpr/ppermute | solution.py:31
  845.4 17.8 %copy-start.3 = (bf16[2,128,4096]{2,1,0:T(8,128)(2,1)S(1)}, bf16[2,128,4096]{2,1,0:T(8,128)(2,1)}, u32[]{:S(2)}) copy-start(bf16[2,128,4096]{2,1,0:T(8,128)(2,1)} %copy-done.2) | copy-start | bytes 6291460 | tf_op jit(solution)/shard_map/while
  845.4 16.8 %collective-permute-start = (bf16[128,4096]{1,0:T(8,128)(2,1)}, bf16[128,4096]{1,0:T(8,128)(2,1)S(1)}, u32[]{:S(2)}, u32[]{:S(2)}) collective-permute-start(bf16[128,4096]{1,0:T(8,128)(2,1)} %get-tuple-element.1077), channel_id=1, source_target_pairs={{0,8},{8,16},{16,24},{1,9},{9,17},{17,25},{2,10},{10,18},{18,26},{... | collective-permute-start | bytes 3145736 | tf_op jit(solution)/shard_map/while/body/eval_jaxpr/ppermute | solution.py:31
  871.0 33.1 %collective-permute-start.1 = (bf16[128,4096]{1,0:T(8,128)(2,1)}, bf16[128,4096]{1,0:T(8,128)(2,1)S(1)}, u32[]{:S(2)}, u32[]{:S(2)}) collective-permute-start(bf16[128,4096]{1,0:T(8,128)(2,1)} %get-tuple-element.1094), channel_id=1, source_target_pairs={{8,0},{16,8},{24,16},{9,1},{17,9},{25,17},{10,2},{18,10},{26,18},{... | collective-permute-start | bytes 3145736 | tf_op jit(solution)/shard_map/while/body/eval_jaxpr/ppermute | solution.py:31
  878.3 25.7 %copy-start.5 = (f32[16,8,4096]{2,1,0:T(8,128)}, f32[16,8,4096]{2,1,0:T(8,128)S(1)}, u32[]{:S(2)}) copy-start(f32[16,8,4096]{2,1,0:T(8,128)S(1)} %get-tuple-element.1191) | copy-start | bytes 6291460 | tf_op jit(solution)/shard_map/while
  907.3 17.0 %collective-permute-start.1 = (bf16[128,4096]{1,0:T(8,128)(2,1)}, bf16[128,4096]{1,0:T(8,128)(2,1)S(1)}, u32[]{:S(2)}, u32[]{:S(2)}) collective-permute-start(bf16[128,4096]{1,0:T(8,128)(2,1)} %get-tuple-element.1094), channel_id=1, source_target_pairs={{8,0},{16,8},{24,16},{9,1},{17,9},{25,17},{10,2},{18,10},{26,18},{... | collective-permute-start | bytes 3145736 | tf_op jit(solution)/shard_map/while/body/eval_jaxpr/ppermute | solution.py:31
  916.2 8.1 copy-start.5
  927.6 62.9 %collective-permute-start.1 = (bf16[128,4096]{1,0:T(8,128)(2,1)}, bf16[128,4096]{1,0:T(8,128)(2,1)S(1)}, u32[]{:S(2)}, u32[]{:S(2)}) collective-permute-start(bf16[128,4096]{1,0:T(8,128)(2,1)} %get-tuple-element.1094), channel_id=1, source_target_pairs={{8,0},{16,8},{24,16},{9,1},{17,9},{25,17},{10,2},{18,10},{26,18},{... | collective-permute-start | bytes 3145736 | tf_op jit(solution)/shard_map/while/body/eval_jaxpr/ppermute | solution.py:31
  936.5 54.0 %copy-start.5 = (f32[16,8,4096]{2,1,0:T(8,128)}, f32[16,8,4096]{2,1,0:T(8,128)S(1)}, u32[]{:S(2)}) copy-start(f32[16,8,4096]{2,1,0:T(8,128)S(1)} %get-tuple-element.1191) | copy-start | bytes 6291460 | tf_op jit(solution)/shard_map/while
  994.4 16.0 %copy-start.30 = (bf16[128,8]{0,1:T(8,128)(2,1)}, bf16[128,8]{0,1:T(8,128)(2,1)S(1)}, u32[]{:S(2)}) copy-start(bf16[128,8]{0,1:T(8,128)(2,1)S(1)} %convolution_convert_fusion.1) | copy-start | bytes 6148 | tf_op jit(solution)/shard_map/while/body/eval_jaxpr/cond
  1017.5 16.3 %collective-permute-start.1 = (bf16[128,4096]{1,0:T(8,128)(2,1)}, bf16[128,4096]{1,0:T(8,128)(2,1)S(1)}, u32[]{:S(2)}, u32[]{:S(2)}) collective-permute-start(bf16[128,4096]{1,0:T(8,128)(2,1)} %get-tuple-element.1094), channel_id=1, source_target_pairs={{8,0},{16,8},{24,16},{9,1},{17,9},{25,17},{10,2},{18,10},{26,18},{... | collective-permute-start | bytes 3145736 | tf_op jit(solution)/shard_map/while/body/eval_jaxpr/ppermute | solution.py:31
  1026.7 7.1 copy-start.5
  1037.0 16.0 %copy-start.25 = (bf16[2,8,4096]{2,0,1:T(2,128)(2,1)S(1)}, bf16[2,8,4096]{2,0,1:T(2,128)(2,1)}, u32[]{:S(2)}) copy-start(bf16[2,8,4096]{2,0,1:T(2,128)(2,1)} %get-tuple-element.856) | copy-start | bytes 393220 | tf_op jit(solution)/shard_map/cond
  1061.6 127.8 %reduce-scatter.3.cloned.1.call-start = ((), (), s32[]{:S(2)}) async-start(), calls=%async_computation.2 | async-start | bytes 1179648 | tf_op jit(solution)/shard_map/reduce_scatter | solution.py:191
  1068.3 122.8 %copy-start.1 = (bf16[1,16,8,4096]{3,2,1,0:T(8,128)(2,1)S(1)}, bf16[1,16,8,4096]{3,2,1,0:T(8,128)(2,1)}, u32[]{:S(2)}) copy-start(bf16[1,16,8,4096]{3,2,1,0:T(8,128)(2,1)} %param.24) | copy-start | bytes 3145732
  (37 other events, 90.8 us)
Sparse Core Ops, SparseCore 0:
  1061.7 60.5 reduce-scatter.4
  1125.7 63.7 reduce-scatter.2
